TPU v7x, 32 devices: a whole 2x2x4 slice. The times are simulated.
32 devices in a mesh: enc: 8 (over z, x), dec: 2 (over y), grp: 2 (over core).
Axes of the slice: x: 2, y: 2, z: 4, core: 2. Of those that a mesh axis runs over, the one named last changes fastest.
Arguments:
- images: bfloat16 [32, 4, 32, 1280], P(('enc', 'dec', 'grp')), may hold values from -6 to 6
- ln_gain: float32 [1280], replicated, may hold values from 0.1 to 1.9
- ln_bias: float32 [1280], replicated, may hold values from -3 to 3
- fc1_weight: bfloat16 [5120, 1280], P('enc'), may hold values from -0.15625 to 0.15625
- fc1_bias: float32 [5120], P('enc'), may hold values from -3 to 3
- fc2_weight: bfloat16 [5120, 1280], P('enc'), may hold values from -0.078125 to 0.078125
- fc2_bias: float32 [1280], replicated, may hold values from -3 to 3
- key_weight: bfloat16 [1280, 512], replicated, may hold values from -0.15625 to 0.15625
- value_weight: bfloat16 [1280, 512], replicated, may hold values from -0.15625 to 0.15625
- text: bfloat16 [32, 128, 8192], P(('enc', 'grp')), may hold values from -6 to 6
- query_weight: bfloat16 [8192, 4096], P('enc', 'dec'), may hold values from -0.0625 to 0.0625
- tiles: int32 [8, 2, 2], replicated, may hold values from 1 to 4, as said below
- links: int32 [32, 2], P(('enc', 'grp')), may hold values from 0 to 1, as said below
- lengths: int32 [32], P(('enc', 'grp')), may hold values from 1 to 128
- state_grads: bfloat16 [32, 4, 32, 1280], P(('enc', 'dec', 'grp')), may hold values from -0.125 to 0.125
Outputs:
- context: bfloat16 [32, 128, 4096], P(('enc', 'grp'), None, 'dec')
- fc1_grad: float32 [5120, 1280], P(('enc', 'dec', 'grp'))
- fc2_grad: float32 [5120, 1280], P(('enc', 'dec', 'grp'))
Inputs may be any that keep to these rules, and one draw needn't show every extreme that they name: The 8 images that share their last two indices have 20 tiles together, and one of them has 4. `links`: every text is linked to at least one image.
All inputs are finite; a program needn't handle non-finite values.
Results may differ from a plain program's by a relative error of at most 0.017.
Values may be sent and summed in bfloat16 or wider, within the bound.
A program may use at most 128 MiB of HBM per device.

v0:
```python
import jax
import jax.numpy as jnp
from jax import lax
from jax.sharding import PartitionSpec as P

HEADS = 32
KV_HEADS = 4
HD = 128


EPSILON = 1e-06


def normalize_layer(values, gain, shift):
    middle = jnp.mean(values, axis=-1, keepdims=True)
    centered = values - middle
    spread = jnp.mean(centered * centered, axis=-1, keepdims=True)
    return centered * lax.rsqrt(spread + EPSILON) * gain + shift


def normalize_heads(values):
    return values * lax.rsqrt(jnp.mean(values * values, axis=-1, keepdims=True) + EPSILON)


def gelu_slope(values):
    return (
        0.5 * (1.0 + lax.erf(values * 0.7071067811865476))
        + values * jnp.exp(-0.5 * values * values) * 0.3989422804014327
    )


def encoder_rows(rows, fc1_weight, fc1_bias, fc2_weight):
    pre = (
        lax.dot_general(
            rows, fc1_weight, (((1,), (1,)), ((), ())), preferred_element_type=jnp.float32
        )
        + fc1_bias
    )
    hidden = jax.nn.gelu(pre, approximate=False).astype(jnp.bfloat16)
    partial_sum = jnp.dot(hidden, fc2_weight, preferred_element_type=jnp.float32)
    return (pre, hidden, partial_sum)


def weight_terms(rows, pre, hidden, cotangent, fc2_weight):
    hidden_grad = lax.dot_general(
        cotangent, fc2_weight, (((1,), (1,)), ((), ())), preferred_element_type=jnp.float32
    )
    second_term = lax.dot_general(
        hidden, cotangent, (((0,), (0,)), ((), ())), preferred_element_type=jnp.float32
    )
    pre_grad = (hidden_grad * gelu_slope(pre)).astype(jnp.bfloat16)
    first_term = lax.dot_general(
        pre_grad, rows, (((0,), (0,)), ((), ())), preferred_element_type=jnp.float32
    )
    return (first_term, second_term)


def project_heads(states, key_columns, value_columns, heads):
    width = states.shape[-1]
    key_raw = jnp.einsum(
        "rd,dhe->hre",
        states,
        key_columns.reshape(width, heads, HD),
        preferred_element_type=jnp.float32,
    )
    keys = normalize_heads(key_raw).astype(jnp.bfloat16)
    values = jnp.einsum(
        "rd,dhe->hre",
        states,
        value_columns.reshape(width, heads, HD),
        preferred_element_type=jnp.float32,
    ).astype(jnp.bfloat16)
    return (keys, values)


def on_device(
    images,
    ln_gain,
    ln_bias,
    fc1_weight,
    fc1_bias,
    fc2_weight,
    fc2_bias,
    key_weight,
    value_weight,
    text,
    query_weight,
    tiles,
    links,
    lengths,
    state_grads,
):
    dec_count = lax.axis_size("dec")
    grp_count = lax.axis_size("grp")
    enc_place = lax.axis_index("enc")
    dec_place = lax.axis_index("dec")
    grp_place = lax.axis_index("grp")
    slots = images.shape[1]
    patch = images.shape[2]
    width = images.shape[3]
    img_rows = slots * patch
    own_rows = images.reshape(img_rows, width)
    normed = normalize_layer(own_rows.astype(jnp.float32), ln_gain, ln_bias).astype(jnp.bfloat16)
    samples = text.shape[0]
    length = text.shape[1]
    text_rows = text.reshape(samples * length, text.shape[2])
    half = query_weight.shape[1] // grp_count
    own_half = lax.dynamic_slice_in_dim(query_weight, grp_place * half, half, 1)
    gathered, half_rows = (
        lax.all_gather(normed, "enc", axis=0, tiled=True),
        lax.all_gather(own_half, "enc", axis=0, tiled=True),
    )
    query_raw = jnp.dot(
        text_rows,
        lax.all_gather(half_rows, "grp", axis=1, tiled=True),
        preferred_element_type=jnp.float32,
    )
    tile_index = jnp.arange(slots)
    pre, hidden, partial_full = encoder_rows(gathered, fc1_weight, fc1_bias, fc2_weight)
    summed = lax.psum_scatter(
        partial_full.astype(jnp.bfloat16), "enc", scatter_dimension=0, tiled=True
    ).astype(jnp.float32)
    states = (own_rows.astype(jnp.float32) + summed + fc2_bias).astype(jnp.bfloat16)
    local_heads = query_weight.shape[1] // HD
    per_group = HEADS // KV_HEADS
    kv_local = max(1, local_heads // per_group)
    first_head = dec_place * local_heads // per_group
    key_columns = lax.dynamic_slice_in_dim(key_weight, first_head * HD, kv_local * HD, 1)
    value_columns = lax.dynamic_slice_in_dim(value_weight, first_head * HD, kv_local * HD, 1)
    piece = lax.all_gather(states.reshape(1, img_rows, width), "dec", axis=0, tiled=True)
    count = piece.shape[0]
    key_part, value_part = project_heads(
        piece.reshape(count * img_rows, width), key_columns, value_columns, kv_local
    )
    key_part = key_part.reshape(kv_local, count, img_rows, HD).transpose(1, 0, 2, 3)
    value_part = value_part.reshape(kv_local, count, img_rows, HD).transpose(1, 0, 2, 3)
    paired = jnp.stack([key_part, value_part])
    keys = paired[0]
    values = paired[1]
    heads_each = local_heads // kv_local
    queries = normalize_heads(query_raw.reshape(samples, length, local_heads, HD)).astype(
        jnp.bfloat16
    )
    queries = queries.reshape(samples, length, kv_local, heads_each, HD)
    dec_tiles = tiles[enc_place, :, grp_place]
    live_keys = tile_index[None, :] < dec_tiles[:, None]
    live_keys = jnp.broadcast_to(live_keys[:, :, None], (dec_count, slots, patch)).reshape(
        dec_count, img_rows
    )
    allowed = (links[:, :, None] > 0) & live_keys[None, :, :]
    scores = jnp.einsum(
        "sqghd,jgkd->sghjkq", queries, keys, preferred_element_type=jnp.float32
    ) * HD ** (-0.5)
    weights = jnp.where(allowed[:, None, None, :, :, None], jnp.exp(scores), 0.0)
    totals = jnp.sum(weights, axis=(3, 4), keepdims=True)
    probs = (weights / totals).astype(jnp.bfloat16)
    mixed = jnp.einsum("sghjkq,jgkd->sqghd", probs, values, preferred_element_type=jnp.float32)
    valid = jnp.arange(length)[None, :] < lengths[:, None]
    context = (
        jnp.where(valid[:, :, None, None, None], mixed, 0.0)
        .reshape(samples, length, local_heads * HD)
        .astype(jnp.bfloat16)
    )
    own_tiles = tiles[enc_place, dec_place, grp_place]
    own_live = jnp.broadcast_to((tile_index < own_tiles)[:, None, None], (slots, patch, 1)).reshape(
        img_rows, 1
    )
    cotangent = jnp.where(
        own_live, state_grads.reshape(img_rows, width), jnp.zeros((), state_grads.dtype)
    )
    all_cotangent = lax.all_gather(cotangent, "enc", axis=0, tiled=True)
    first_term, second_term = weight_terms(gathered, pre, hidden, all_cotangent, fc2_weight)
    fc1_grad, fc2_grad = (
        lax.psum_scatter(
            first_term.astype(jnp.bfloat16), ("dec", "grp"), scatter_dimension=0, tiled=True
        ).astype(jnp.float32),
        lax.psum_scatter(
            second_term.astype(jnp.bfloat16), ("dec", "grp"), scatter_dimension=0, tiled=True
        ).astype(jnp.float32),
    )
    return (context, fc1_grad, fc2_grad)


def solution(mesh):
    in_specs = (
        P(("enc", "dec", "grp"), None, None, None),
        P(),
        P(),
        P("enc", None),
        P("enc"),
        P("enc", None),
        P(),
        P(),
        P(),
        P(("enc", "grp"), None, None),
        P("enc", "dec"),
        P(),
        P(("enc", "grp"), None),
        P(("enc", "grp")),
        P(("enc", "dec", "grp"), None, None, None),
    )
    out_specs = (
        P(("enc", "grp"), None, "dec"),
        P(("enc", "dec", "grp"), None),
        P(("enc", "dec", "grp"), None),
    )
    return jax.shard_map(
        on_device, mesh=mesh, in_specs=in_specs, out_specs=out_specs, check_vma=False
    )
```

profile of v0, /device:TPU:0, one launch (start us, length us, event | category | flops | bytes accessed | tf_op | source)
XLA Modules:
  0.0 579.2 jit_solution(997100307381949104)
XLA Ops:
  7.2 0.0 copy-start
  7.2 0.0 all-gather.6.cloned.1.call-start
  7.2 1.2 convert_reduce_fusion
  8.4 0.1 div.40
  8.5 1.2 fusion.29
  9.8 0.1 rsqrt.31
  9.8 2.0 fusion.33
  11.8 0.0 all-gather.6.cloned.1.call-update
  11.8 0.0 all-gather.12.cloned.1.call-start
  11.9 1.3 dynamic_slice.19
  13.2 0.6 iota_compare_fusion.2
  13.8 0.1 broadcast_in_dim.70
  13.9 0.1 broadcast_in_dim.71
  14.0 1.8 bitcast_select_fusion.2
  15.8 0.0 all-gather.12.cloned.1.call-update
  15.8 0.0 all-gather.8.cloned.1.call-start
  15.9 3.3 constant_dynamic-slice_fusion
  19.2 0.0 all-gather.8.cloned.1.call-update
  19.2 0.0 reduce-scatter.6.cloned.1.call-start
  19.2 49.9 %all-gather.6.cloned.1.call-done = bf16[1024,1280]{1,0:T(8,128)(2,1)} async-done(((bf16[128,1280]{1,0:T(8,128)(2,1)}), bf16[1024,1280]{1,0:T(8,128)(2,1)}) %all-gather.6.cloned.1.call-update) | async-done | bytes 2621456 | tf_op jit(solution)/shard_map/all_gather | solution.py:110
  69.1 10.1 %fusion.3 = (bf16[1024,640]{1,0:T(8,128)(2,1)}, f32[1024,640]{1,0:T(8,128)}) fusion(f32[640]{0:T(1024)S(1)} %copy-done.6, bf16[1024,1280]{1,0:T(8,128)(2,1)} %all-gather.6.cloned.1.call-done, bf16[640,1280]{1,0:T(8,128)(2,1)S(1)} %copy-done.5), kind=kOutput, calls=%fused_computation.11 | convolution fusion | flops 1720975360 | bytes 8194560 | tf_op jit(solution)/shard_map/dot_general | solution.py:34
  79.2 45.7 %all-gather.12.cloned.1.call-done = bf16[1024,1280]{1,0:T(8,128)(2,1)} async-done(((bf16[128,1280]{1,0:T(8,128)(2,1)}), bf16[1024,1280]{1,0:T(8,128)(2,1)}) %all-gather.12.cloned.1.call-update) | async-done | bytes 2621456 | tf_op jit(solution)/shard_map/all_gather | solution.py:171
  124.9 11.8 %convolution_convert_fusion.2 = bf16[640,1280]{1,0:T(8,128)(2,1)} fusion(bf16[1024,1280]{1,0:T(8,128)(2,1)} %all-gather.6.cloned.1.call-done, f32[1024,640]{1,0:T(8,128)} %get-tuple-element.13, bf16[1024,1280]{1,0:T(8,128)(2,1)} %all-gather.12.cloned.1.call-done, bf16[640,1280]{1,0:T(8,128)(2,1)S(1)} %copy-done, f32[640]{0:T(1024)S(1)} %copy-done.6), kind=kOutput, calls=%fused_computation.7 | convolution fusion | flops 3363471360 | bytes 11143680 | tf_op jit(solution)/shard_map/dot_general | solution.py:52
  136.7 0.0 reduce-scatter.6.cloned.1.call-update
  136.7 0.0 reduce-scatter.8.cloned.1.call-start
  136.7 5.2 convolution_convert_fusion.1
  142.0 0.0 reduce-scatter.8.cloned.1.call-update
  142.0 0.2 reduce-scatter.4.cloned.1.call-start
  142.2 3.7 convolution_convert_fusion
  145.9 0.0 reduce-scatter.4.cloned.1.call-update
  145.9 0.0 all-gather.10.cloned.1.call-start
  146.0 206.9 %all-gather.8.cloned.1.call-done = bf16[8192,1024]{1,0:T(8,128)(2,1)} async-done(((bf16[1024,1024]{1,0:T(8,128)(2,1)}), bf16[8192,1024]{1,0:T(8,128)(2,1)}) %all-gather.8.cloned.1.call-update) | async-done | bytes 16777232 | tf_op jit(solution)/shard_map/all_gather | solution.py:111
  352.9 0.0 all-gather.10.cloned.1.call-update
  353.0 0.6 copy-done.7
  353.6 0.1 copy.48
  353.7 0.2 dynamic-slice_reduce_fusion
  353.9 0.1 iota_compare_fusion
  354.0 0.1 broadcast_in_dim.39
  354.1 0.1 and.29
  354.1 1.4 constant_dynamic-slice_fusion.1
  355.6 0.2 copy.49
  355.8 0.2 copy.46
  356.1 0.1 iota_compare_fusion.1
  356.1 0.1 broadcast_and_fusion
  356.2 25.8 %reduce-scatter.6.cloned.1.call-done = bf16[160,1280]{1,0:T(8,128)(2,1)} async-done(((bf16[640,1280]{1,0:T(8,128)(2,1)}), bf16[160,1280]{1,0:T(8,128)(2,1)}) %reduce-scatter.6.cloned.1.call-update) | async-done | bytes 409616 | tf_op jit(solution)/shard_map/reduce_scatter | solution.py:174
  382.0 1.9 convert_element_type.88
  384.0 28.9 %reduce-scatter.8.cloned.1.call-done = bf16[160,1280]{1,0:T(8,128)(2,1)} async-done(((bf16[640,1280]{1,0:T(8,128)(2,1)}), bf16[160,1280]{1,0:T(8,128)(2,1)}) %reduce-scatter.8.cloned.1.call-update) | async-done | bytes 409616 | tf_op jit(solution)/shard_map/reduce_scatter | solution.py:177
  412.8 1.9 convert_element_type.90
  414.8 72.4 %reduce-scatter.4.cloned.1.call-done = bf16[128,1280]{1,0:T(8,128)(2,1)} async-done(((bf16[1024,1280]{1,0:T(8,128)(2,1)}), bf16[128,1280]{1,0:T(8,128)(2,1)}) %reduce-scatter.4.cloned.1.call-update) | async-done | bytes 327696 | tf_op jit(solution)/shard_map/reduce_scatter | solution.py:120
  487.2 1.1 fusion.35
  488.3 8.7 %all-gather = bf16[256,1280]{1,0:T(8,128)(2,1)S(1)} all-gather(bf16[128,1280]{1,0:T(8,128)(2,1)S(1)} %fusion.35), channel_id=2, replica_groups=mesh['enc'=8,'dec'=2,'grp'=2] {'dec'}, dimensions={0}, use_global_device_ids=true | all-gather | bytes 983040 | tf_op jit(solution)/shard_map/all_gather | solution.py:130
  497.0 0.4 multiply_reduce_fusion
  497.4 0.1 copy.61
  497.5 0.4 fusion.20
  497.9 41.0 %all-gather.10.cloned.1.call-done = bf16[8192,2048]{1,0:T(8,128)(2,1)} async-done(((bf16[8192,1024]{1,0:T(8,128)(2,1)}), bf16[8192,2048]{1,0:T(8,128)(2,1)}) %all-gather.10.cloned.1.call-update) | async-done | bytes 33554448 | tf_op jit(solution)/shard_map/all_gather | solution.py:115
  538.9 17.7 %fusion.48 = (f32[256,2048]{0,1:T(8,128)}, f32[256,2048]{0,1:T(8,128)}) fusion(bf16[8192,2048]{1,0:T(8,128)(2,1)} %all-gather.10.cloned.1.call-done, bf16[256,8192]{1,0:T(8,128)(2,1)} %bitcast.111), kind=kOutput, calls=%fused_computation.87 | convolution fusion | flops 8590458880 | bytes 41943040 | tf_op jit(solution)/shard_map/dot_general | solution.py:113
  556.6 2.3 mul.116
  558.9 3.3 reshape.170
  562.2 4.1 copy.53
  566.3 0.6 reduce_sum.48
  566.9 2.9 fusion
  569.8 1.2 fusion.19
  571.0 0.1 copy.55
  571.1 1.3 copy.56
  (23 shorter events, 0.1 us)
Async XLA Ops:
  7.2 117.7 %copy-start = (bf16[640,1280]{1,0:T(8,128)(2,1)S(1)}, bf16[640,1280]{1,0:T(8,128)(2,1)}, u32[]{:S(2)}) copy-start(bf16[640,1280]{1,0:T(8,128)(2,1)} %param.20) | copy-start | bytes 4915204
  7.2 61.9 %all-gather.6.cloned.1.call-start = ((), (), s32[]{:S(2)}) async-start(), calls=%async_computation.3 | async-start | bytes 2949120 | tf_op jit(solution)/shard_map/all_gather | solution.py:110
  11.8 113.0 %all-gather.12.cloned.1.call-start = ((), (), s32[]{:S(2)}) async-start(), calls=%async_computation.7 | async-start | bytes 2949120 | tf_op jit(solution)/shard_map/all_gather | solution.py:171
  15.8 337.1 %all-gather.8.cloned.1.call-start = ((), (), s32[]{:S(2)}) async-start(), calls=%async_computation.5 | async-start | bytes 18874368 | tf_op jit(solution)/shard_map/all_gather | solution.py:111
  15.9 53.3 %copy-start.5 = (bf16[640,1280]{1,0:T(8,128)(2,1)S(1)}, bf16[640,1280]{1,0:T(8,128)(2,1)}, u32[]{:S(2)}) copy-start(bf16[640,1280]{1,0:T(8,128)(2,1)} %param.18) | copy-start | bytes 4915204
  15.9 53.3 %copy-start.6 = (f32[640]{0:T(1024)S(1)}, f32[640]{0:T(1024)}, u32[]{:S(2)}) copy-start(f32[640]{0:T(1024)} %param.19) | copy-start | bytes 7684
  19.2 362.8 %reduce-scatter.6.cloned.1.call-start = ((), (), s32[]{:S(2)}) async-start(), calls=%async_computation.8 | async-start | bytes 2048000 | tf_op jit(solution)/shard_map/reduce_scatter | solution.py:174
  124.9 11.8 %copy-start.9 = (bf16[1024,640]{1,0:T(8,128)(2,1)S(1)}, bf16[1024,640]{1,0:T(8,128)(2,1)}, u32[]{:S(2)}) copy-start(bf16[1024,640]{1,0:T(8,128)(2,1)} %get-tuple-element.12) | copy-start | bytes 3932164
  136.7 276.2 %reduce-scatter.8.cloned.1.call-start = ((), (), s32[]{:S(2)}) async-start(), calls=%async_computation.9 | async-start | bytes 2048000 | tf_op jit(solution)/shard_map/reduce_scatter | solution.py:177
  142.0 345.2 %reduce-scatter.4.cloned.1.call-start = ((), (), s32[]{:S(2)}) async-start(), calls=%async_computation.4 | async-start | bytes 2949120 | tf_op jit(solution)/shard_map/reduce_scatter | solution.py:120
  145.9 393.0 %all-gather.10.cloned.1.call-start = ((), (), s32[]{:S(2)}) async-start(), calls=%async_computation.6 | async-start | bytes 50331648 | tf_op jit(solution)/shard_map/all_gather | solution.py:115
  352.9 0.7 copy-start.7
  352.9 0.8 copy-start.4
  354.1 1.9 copy-start.8
  355.5 131.6 %copy-start.2 = (bf16[1,4,32,1280]{3,2,1,0:T(8,128)(2,1)S(1)}, bf16[1,4,32,1280]{3,2,1,0:T(8,128)(2,1)}, u32[]{:S(2)}) copy-start(bf16[1,4,32,1280]{3,2,1,0:T(8,128)(2,1)} %param.15) | copy-start | bytes 983044
  355.6 131.6 %copy-start.3 = (f32[1280]{0:T(1024)S(1)}, f32[1280]{0:T(1024)}, u32[]{:S(2)}) copy-start(f32[1280]{0:T(1024)} %param.21) | copy-start | bytes 15364
  569.8 2.6 copy-start.1
Sparse Core Ops, SparseCore 0:
  12.0 57.1 all-gather.5
  71.9 52.9 all-gather.11
  127.0 225.8 all-gather.7
  355.3 26.6 reduce-scatter.5
  384.4 28.3 reduce-scatter.7
  416.2 70.9 reduce-scatter.3
  488.7 50.1 all-gather.9
where the time goes:
time: 580 us; the launch traced here: 579 us
  waiting for transfers between devices  471 us (81%)
  matrix products  53.3 us (9%)
  local copies, waits for them, and re-layouts  19.1 us (3%)
  between operations  14.3 us (2%)
  other arithmetic  12.6 us (2%)
  blocking collectives  8.7 us (1%)
    all_gather x1, waiting for transfers between devices, on_device(): lax.all_gather(own_half, 'enc', axis=0, tiled=True)  207 us
    reduce_scatter x1, waiting for transfers between devices, on_device(): lax.psum_scatter(partial_full.astype(jnp.bfloat16), 'enc', scatter_dimens...  72.4 us
    all_gather x1, waiting for transfers between devices, on_device(): lax.all_gather(normed, 'enc', axis=0, tiled=True)  49.9 us
    all_gather x1, waiting for transfers between devices, on_device(): all_cotangent = lax.all_gather(cotangent, 'enc', axis=0, tiled=True)  45.7 us
    all_gather x1, waiting for transfers between devices, on_device(): lax.all_gather(half_rows, 'grp', axis=1, tiled=True)  41 us
    reduce_scatter x1, waiting for transfers between devices, on_device(): lax.psum_scatter(second_term.astype(jnp.bfloat16), ('dec', 'grp'), scatte...  28.9 us
    reduce_scatter x1, waiting for transfers between devices, on_device(): lax.psum_scatter(first_term.astype(jnp.bfloat16), ('dec', 'grp'), scatter...  25.8 us
    dot_general x1, matrix products, on_device(): jnp.dot(text_rows, lax.all_gather(half_rows, 'grp', axis=1, tiled=True),...  17.7 us
  transfers between devices with their start and end apart: 7, of which 7 were waited for; matrix products, arithmetic and copies ran while one was open for 8% of the time, Pallas kernels for 0%

commit v1 on v0

--- a/solution.py
+++ b/solution.py
@@ -71,6 +71,103 @@
         preferred_element_type=jnp.float32,
     ).astype(jnp.bfloat16)
     return (keys, values)
+
+def shifted(values, axis, step):
+    size = lax.axis_size(axis)
+    return lax.ppermute(values, axis, [(i, (i + step) % size) for i in range(size)])
+
+
+def swapped(values):
+    return lax.ppermute(values, "enc", [(i, i ^ 1) for i in range(lax.axis_size("enc"))])
+
+
+def share_text(text_rows):
+    enc_count = lax.axis_size("enc")
+    rows, depth = text_rows.shape
+    side = lax.axis_index("enc") % 2
+    block = depth // enc_count
+    parts = text_rows.reshape(rows, enc_count // 2, 2, block)
+    own = lax.dynamic_index_in_dim(parts, side, 2, keepdims=False).transpose(1, 0, 2)
+    away = lax.dynamic_index_in_dim(parts, 1 - side, 2, keepdims=False).transpose(1, 0, 2)
+    pair = jnp.concatenate([swapped(away), own], axis=1)
+    return jnp.concatenate(
+        [pair] + [shifted(pair, "grp", step) for step in range(1, lax.axis_size("grp"))], axis=1
+    )
+
+
+def project_queries(text_blocks, weight):
+    grp_count = lax.axis_size("grp")
+    ring = lax.axis_size("enc") // 2
+    enc_count = lax.axis_size("enc")
+    place = lax.axis_index("enc") // 2
+    total = None
+    for step in range(ring):
+        left = lax.dynamic_index_in_dim(text_blocks, (place - step) % ring, 0, keepdims=False)
+        term = jnp.dot(left, weight, preferred_element_type=jnp.float32)
+        total = term if total is None else total + term
+        if step < ring - 1:
+            weight = lax.ppermute(
+                weight, "enc", [(i, (i + 2) % enc_count) for i in range(enc_count)]
+            )
+    columns = total.shape[1]
+    total = total.reshape(grp_count, 2, -1, columns)
+    arrived = swapped(total[:, 0].astype(jnp.bfloat16))
+    raw = total[:, 1] + arrived.astype(jnp.float32)
+    own = normalize_heads(raw.reshape(grp_count, -1, columns // HD, HD)).astype(jnp.bfloat16)
+    blocks = jnp.stack(
+        [own[0]] + [shifted(own[step], "grp", -step) for step in range(1, grp_count)], axis=1
+    )
+    start = (grp_count - lax.axis_index("grp")) % grp_count
+    blocks = lax.dynamic_slice_in_dim(
+        jnp.concatenate([blocks, blocks], axis=1), start, grp_count, 1
+    )
+    return blocks.reshape(blocks.shape[0], grp_count * columns)
+
+
+def share_keys(states, key_weight, value_weight, first_head, kv_local):
+    dec_count = lax.axis_size("dec")
+    rows, width = states.shape
+    if dec_count == 2 and kv_local * dec_count == KV_HEADS:
+        keys, values = project_heads(states, key_weight, value_weight, KV_HEADS)
+        paired = jnp.stack([keys, values])
+        own = lax.dynamic_slice_in_dim(paired, first_head, kv_local, 1)
+        away = lax.dynamic_slice_in_dim(paired, KV_HEADS - kv_local - first_head, kv_local, 1)
+        arrived = shifted(away, "dec", 1)
+        first = lax.axis_index("dec") == 0
+        paired = jnp.stack(
+            [jnp.where(first, own, arrived), jnp.where(first, arrived, own)], axis=1
+        )
+        return (paired[0], paired[1])
+    key_columns = lax.dynamic_slice_in_dim(key_weight, first_head * HD, kv_local * HD, 1)
+    value_columns = lax.dynamic_slice_in_dim(value_weight, first_head * HD, kv_local * HD, 1)
+    piece = lax.all_gather(states, "dec", axis=0, tiled=True)
+    key_part, value_part = project_heads(piece, key_columns, value_columns, kv_local)
+    shape = (kv_local, dec_count, rows, HD)
+    return (
+        key_part.reshape(shape).transpose(1, 0, 2, 3),
+        value_part.reshape(shape).transpose(1, 0, 2, 3),
+    )
+
+
+def share_grads(terms):
+    dec_count = lax.axis_size("dec")
+    grp_count = lax.axis_size("grp")
+    rows = terms.shape[1] // (dec_count * grp_count)
+    if dec_count == 2 and grp_count == 2:
+        parts = terms.reshape(2, dec_count, grp_count, rows, -1)
+        grp_place = lax.axis_index("grp")
+        dec_place = lax.axis_index("dec")
+        kept = lax.dynamic_index_in_dim(parts, grp_place, 2, keepdims=False)
+        away = lax.dynamic_index_in_dim(parts, 1 - grp_place, 2, keepdims=False)
+        kept = kept + shifted(away.astype(jnp.bfloat16), "grp", 1).astype(jnp.float32)
+        away = lax.dynamic_index_in_dim(kept, 1 - dec_place, 1, keepdims=False)
+        kept = lax.dynamic_index_in_dim(kept, dec_place, 1, keepdims=False)
+        kept = kept + shifted(away.astype(jnp.bfloat16), "dec", 1).astype(jnp.float32)
+        return (kept[0], kept[1])
+    summed = lax.psum_scatter(
+        terms.astype(jnp.bfloat16), ("dec", "grp"), scatter_dimension=1, tiled=True
+    ).astype(jnp.float32)
+    return (summed[0], summed[1])
 
 
 def on_device(
@@ -106,16 +203,18 @@
     text_rows = text.reshape(samples * length, text.shape[2])
     half = query_weight.shape[1] // grp_count
     own_half = lax.dynamic_slice_in_dim(query_weight, grp_place * half, half, 1)
-    gathered, half_rows = (
-        lax.all_gather(normed, "enc", axis=0, tiled=True),
-        lax.all_gather(own_half, "enc", axis=0, tiled=True),
-    )
-    query_raw = jnp.dot(
-        text_rows,
-        lax.all_gather(half_rows, "grp", axis=1, tiled=True),
-        preferred_element_type=jnp.float32,
-    )
+    own_tiles = tiles[enc_place, dec_place, grp_place]
     tile_index = jnp.arange(slots)
+    own_live = jnp.broadcast_to((tile_index < own_tiles)[:, None, None], (slots, patch, 1)).reshape(
+        img_rows, 1
+    )
+    cotangent = jnp.where(
+        own_live, state_grads.reshape(img_rows, width), jnp.zeros((), state_grads.dtype)
+    )
+    both = lax.all_gather(jnp.stack([normed, cotangent]), "enc", axis=1, tiled=True)
+    gathered, all_cotangent = both[0], both[1]
+    text_blocks = share_text(text_rows)
+    queries_of = project_queries(text_blocks, own_half)
     pre, hidden, partial_full = encoder_rows(gathered, fc1_weight, fc1_bias, fc2_weight)
     summed = lax.psum_scatter(
         partial_full.astype(jnp.bfloat16), "enc", scatter_dimension=0, tiled=True
@@ -125,22 +224,9 @@
     per_group = HEADS // KV_HEADS
     kv_local = max(1, local_heads // per_group)
     first_head = dec_place * local_heads // per_group
-    key_columns = lax.dynamic_slice_in_dim(key_weight, first_head * HD, kv_local * HD, 1)
-    value_columns = lax.dynamic_slice_in_dim(value_weight, first_head * HD, kv_local * HD, 1)
-    piece = lax.all_gather(states.reshape(1, img_rows, width), "dec", axis=0, tiled=True)
-    count = piece.shape[0]
-    key_part, value_part = project_heads(
-        piece.reshape(count * img_rows, width), key_columns, value_columns, kv_local
-    )
-    key_part = key_part.reshape(kv_local, count, img_rows, HD).transpose(1, 0, 2, 3)
-    value_part = value_part.reshape(kv_local, count, img_rows, HD).transpose(1, 0, 2, 3)
-    paired = jnp.stack([key_part, value_part])
-    keys = paired[0]
-    values = paired[1]
+    keys, values = share_keys(states, key_weight, value_weight, first_head, kv_local)
     heads_each = local_heads // kv_local
-    queries = normalize_heads(query_raw.reshape(samples, length, local_heads, HD)).astype(
-        jnp.bfloat16
-    )
+    queries = queries_of
     queries = queries.reshape(samples, length, kv_local, heads_each, HD)
     dec_tiles = tiles[enc_place, :, grp_place]
     live_keys = tile_index[None, :] < dec_tiles[:, None]
@@ -161,23 +247,8 @@
         .reshape(samples, length, local_heads * HD)
         .astype(jnp.bfloat16)
     )
-    own_tiles = tiles[enc_place, dec_place, grp_place]
-    own_live = jnp.broadcast_to((tile_index < own_tiles)[:, None, None], (slots, patch, 1)).reshape(
-        img_rows, 1
-    )
-    cotangent = jnp.where(
-        own_live, state_grads.reshape(img_rows, width), jnp.zeros((), state_grads.dtype)
-    )
-    all_cotangent = lax.all_gather(cotangent, "enc", axis=0, tiled=True)
     first_term, second_term = weight_terms(gathered, pre, hidden, all_cotangent, fc2_weight)
-    fc1_grad, fc2_grad = (
-        lax.psum_scatter(
-            first_term.astype(jnp.bfloat16), ("dec", "grp"), scatter_dimension=0, tiled=True
-        ).astype(jnp.float32),
-        lax.psum_scatter(
-            second_term.astype(jnp.bfloat16), ("dec", "grp"), scatter_dimension=0, tiled=True
-        ).astype(jnp.float32),
-    )
+    fc1_grad, fc2_grad = share_grads(jnp.stack([first_term, second_term]))
     return (context, fc1_grad, fc2_grad)
 
 

time: 580 us -> 361 us (0.62)
  waiting for transfers between devices: 471 us -> 208 us
  local copies, waits for them, and re-layouts: 19.1 us -> 42.7 us
  starting transfers between devices: 0.47 us -> 20.5 us
  other arithmetic: 12.6 us -> 24.5 us
  blocking collectives: 8.7 us -> 0 us
    all_gather x4 -> x1, waiting for transfers between devices: 344 us -> 0.01 us  [on_device(): lax.all_gather(jnp.stack([normed, cotangent]), 'enc', axis=1, tiled=True)]
    ppermute x0 -> x10, waiting for transfers between devices: none -> 189 us  [the longest x3 127 us: project_queries(): lax.ppermute(weight, 'enc', [(i, (i + 2) % enc_count) for i in range(enc_...]
    reduce_scatter x2 -> x0, waiting for transfers between devices: 54.7 us -> none  [the longest x1 28.9 us: on_device(): lax.psum_scatter(second_term.astype(jnp.bfloat16), ('dec', 'grp'), scatte...]
    reduce_scatter x1, waiting for transfers between devices: 72.4 us -> 18.7 us  [on_device(): lax.psum_scatter(partial_full.astype(jnp.bfloat16), 'enc', scatter_dimens...]
    ppermute x0 -> x10, starting transfers between devices: none -> 20.4 us  [the longest x3 12.9 us: project_queries(): lax.ppermute(weight, 'enc', [(i, (i + 2) % enc_count) for i in range(enc_...]
    dynamic_slice x3, local copies, waits for them, and re-layouts: 1.88 us -> 19.1 us  [the longest x2 16.8 us: share_text(): lax.dynamic_index_in_dim(parts, 1 - side, 2, keepdims=False)]
    concatenate x0 -> x3, other arithmetic: none -> 9.88 us  [the longest x1 4.16 us: share_text(): jnp.concatenate([pair] + [shifted(pair, 'grp', step) for step in range(1,...]
    all_gather x1 -> x0, blocking collectives: 8.7 us -> none  [on_device(): lax.all_gather(states.reshape(1, img_rows, width), 'dec', axis=0, tiled=T...]
  transfers between devices with their start and end apart: 7 -> 12, of which waited for: 7 -> 7; matrix products, arithmetic and copies ran while one was open for 8% -> 22% of each run, Pallas kernels for 0% -> 0%
where the time goes in v1:
time: 361 us; the launch traced here: 360 us
  waiting for transfers between devices  208 us (58%)
  matrix products  50 us (14%)
  local copies, waits for them, and re-layouts  42.7 us (12%)
  other arithmetic  24.5 us (7%)
  starting transfers between devices  20.5 us (6%)
  between operations  14.5 us (4%)
    ppermute x3, waiting for transfers between devices, project_queries(): lax.ppermute(weight, 'enc', [(i, (i + 2) % enc_count) for i in range(enc_...  127 us
    ppermute x2, waiting for transfers between devices, swapped(): lax.ppermute(values, 'enc', [(i, i ^ 1) for i in range(lax.axis_size('enc...  43.8 us
    ppermute x5, waiting for transfers between devices, shifted(): lax.ppermute(values, axis, [(i, (i + step) % size) for i in range(size)])  18.9 us
    reduce_scatter x1, waiting for transfers between devices, on_device(): lax.psum_scatter(partial_full.astype(jnp.bfloat16), 'enc', scatter_dimens...  18.7 us
    dynamic_slice x2, local copies, waits for them, and re-layouts, share_text(): lax.dynamic_index_in_dim(parts, 1 - side, 2, keepdims=False)  16.8 us
    ppermute x3, starting transfers between devices, project_queries(): lax.ppermute(weight, 'enc', [(i, (i + 2) % enc_count) for i in range(enc_...  12.9 us
    dot_general x4, matrix products, project_queries(): term = jnp.dot(left, weight, preferred_element_type=jnp.float32)  12.6 us
    dot_general x1, matrix products, encoder_rows(): lax.dot_general(rows, fc1_weight, (((1,), (1,)), ((), ())), preferred_ele...  10.1 us
  transfers between devices with their start and end apart: 12, of which 7 were waited for; matrix products, arithmetic and copies ran while one was open for 22% of the time, Pallas kernels for 0%

profile of v1, /device:TPU:0, one launch (start us, length us, event | category | flops | bytes accessed | tf_op | source)
XLA Modules:
  0.0 360.4 jit_solution(2464812177278716316)
XLA Ops:
  7.2 7.9 %reshape_reshape.6 = bf16[256,4,2,1024]{3,2,1,0:T(2,128)(2,1)} reshape(bf16[2,128,8192]{2,1,0:T(8,128)(2,1)} %param.24) | data formatting | bytes 8388608 | tf_op jit(solution)/shard_map/reshape;reshape | solution.py:89
  15.2 13.3 %constant_dynamic-slice_fusion.2 = (bf16[256,4,1,1024]{3,2,1,0:T(2,128)(2,1)S(1)}, bf16[256,4,1,1024]{3,2,1,0:T(2,128)(2,1)}) fusion(bf16[256,4,2,1024]{3,2,1,0:T(2,128)(2,1)} %reshape_reshape.6, s32[]{:T(128)S(6)} %select_n.130, s32[]{:T(128)S(6)} %select_n.131), kind=kLoop, calls=%fused_computation.200 | loop fusion | bytes 8388616 | tf_op jit(solution)/shard_map/jit(dynamic_index_in_dim)/dynamic_slice | solution.py:91
  28.5 3.5 copy.131
  32.0 3.0 collective-permute-start.1
  35.0 0.1 convert_reduce_fusion
  35.2 0.2 multiply_reduce_fusion
  35.5 0.6 dynamic_slice.52
  36.1 0.6 iota_compare_fusion.2
  36.8 0.1 broadcast_in_dim.40
  37.0 0.1 bitcast_select_fusion.2
  37.1 0.3 fusion.128
  37.4 0.9 pad_maximum_fusion.2
  38.4 1.9 constant_dynamic-slice_fusion
  40.3 1.6 collective-permute-start.3
  41.9 2.2 copy.130
  44.2 43.8 %collective-permute-done.1 = bf16[4,256,1024]{2,1,0:T(8,128)(2,1)} collective-permute-done((bf16[4,256,1024]{2,1,0:T(8,128)(2,1)}, bf16[4,256,1024]{2,1,0:T(8,128)(2,1)}, u32[]{:S(2)}, u32[]{:S(2)}) %collective-permute-start.1) | collective-permute-done | bytes 2097184 | tf_op jit(solution)/shard_map/ppermute | solution.py:81
  88.0 4.1 %pad_maximum_fusion.1 = bf16[4,512,1024]{2,1,0:T(8,128)(2,1)} fusion(bf16[4,256,1024]{2,1,0:T(8,128)(2,1)S(1)} %bitcast.237, bf16[4,256,1024]{2,1,0:T(8,128)(2,1)} %collective-permute-done.1), kind=kLoop, calls=%fused_computation.5 | loop fusion | flops 8388608 | bytes 8388608 | tf_op jit(solution)/shard_map/concatenate | solution.py:92
  92.1 28.4 %collective-permute-done.3 = bf16[1024,1024]{1,0:T(8,128)(2,1)} collective-permute-done((bf16[1024,1024]{1,0:T(8,128)(2,1)S(1)}, bf16[1024,1024]{1,0:T(8,128)(2,1)}, u32[]{:S(2)}, u32[]{:S(2)}) %collective-permute-start.3) | collective-permute-done | bytes 2097184 | tf_op jit(solution)/shard_map/ppermute | solution.py:109
  120.5 11.2 %collective-permute-start.4 = (bf16[1024,1024]{1,0:T(8,128)(2,1)}, bf16[1024,1024]{1,0:T(8,128)(2,1)}, u32[]{:S(2)}, u32[]{:S(2)}) collective-permute-start(bf16[1024,1024]{1,0:T(8,128)(2,1)} %collective-permute-done.3), channel_id=1, source_target_pairs={{0,8},{4,12},{8,16},{12,20},{16,24},{20,28},{24,0},{28,4},{1,9},{5... | collective-permute-start | bytes 6291464 | tf_op jit(solution)/shard_map/ppermute | solution.py:109
  131.7 66.1 %collective-permute-done.4 = bf16[1024,1024]{1,0:T(8,128)(2,1)} collective-permute-done((bf16[1024,1024]{1,0:T(8,128)(2,1)}, bf16[1024,1024]{1,0:T(8,128)(2,1)}, u32[]{:S(2)}, u32[]{:S(2)}) %collective-permute-start.4) | collective-permute-done | bytes 2097184 | tf_op jit(solution)/shard_map/ppermute | solution.py:109
  197.8 4.2 %pad_maximum_fusion = bf16[4,1024,1024]{2,1,0:T(8,128)(2,1)S(1)} fusion(bf16[4,512,1024]{2,1,0:T(8,128)(2,1)} %collective-permute-done.2, bf16[4,256,1024]{2,1,0:T(8,128)(2,1)} %bitcast.238, bf16[4,256,1024]{2,1,0:T(8,128)(2,1)} %collective-permute-done.1), kind=kLoop, calls=%fused_computation | loop fusion | flops 25165824 | bytes 16777216 | tf_op jit(solution)/shard_map/concatenate | solution.py:93
  202.0 2.3 fusion.59
  204.3 3.9 %fusion.55 = f32[1024,1024]{1,0:T(8,128)S(1)} fusion(bf16[1024,1024]{1,0:T(8,128)(2,1)} %collective-permute-done.4, bf16[4,1024,1024]{2,1,0:T(8,128)(2,1)S(1)} %pad_maximum_fusion, s32[]{:T(128)S(6)} %select_n.139), kind=kOutput, calls=%fused_computation.96 | convolution fusion | flops 2147483648 | bytes 8388612 | tf_op jit(solution)/shard_map/dot_general | solution.py:106
  208.2 3.9 %fusion.57 = f32[1024,1024]{1,0:T(8,128)S(1)} fusion(bf16[1024,1024]{1,0:T(8,128)(2,1)} %collective-permute-done.3, bf16[4,1024,1024]{2,1,0:T(8,128)(2,1)S(1)} %pad_maximum_fusion, s32[]{:T(128)S(6)} %select_n.137), kind=kOutput, calls=%fused_computation.98 | convolution fusion | flops 2147483648 | bytes 8388612 | tf_op jit(solution)/shard_map/dot_general | solution.py:106
  212.2 32.2 %collective-permute-done.5 = bf16[1024,1024]{1,0:T(8,128)(2,1)S(1)} collective-permute-done((bf16[1024,1024]{1,0:T(8,128)(2,1)}, bf16[1024,1024]{1,0:T(8,128)(2,1)S(1)}, u32[]{:S(2)}, u32[]{:S(2)}) %collective-permute-start.5) | collective-permute-done | bytes 2097184 | tf_op jit(solution)/shard_map/ppermute | solution.py:109
  244.4 2.4 add_add_fusion
  246.9 2.0 copy-done.7
  248.9 1.1 fusion.121
  250.0 0.9 collective-permute-start.6
  250.9 10.1 %fusion.17 = (bf16[640,1024]{1,0:T(8,128)(2,1)}, f32[1024,640]{0,1:T(8,128)S(1)}) fusion(f32[640]{0:T(1024)S(1)} %copy-done.19, bf16[640,1280]{1,0:T(8,128)(2,1)} %param.18, bf16[2,1024,1280]{2,1,0:T(8,128)(2,1)} %all-gather.2.cloned.1.call-done), kind=kOutput, calls=%fused_computation.32 | convolution fusion | flops 1720975360 | bytes 8194560 | tf_op jit(solution)/shard_map/dot_general | solution.py:34
  261.0 1.5 copy-done.23
  262.5 8.9 %convolution_convert_fusion = bf16[1024,1280]{1,0:T(8,128)(2,1)} fusion(bf16[640,1280]{1,0:T(8,128)(2,1)S(1)} %copy-done, f32[1024,640]{0,1:T(8,128)S(1)} %get-tuple-element.30, f32[640]{0:T(1024)S(1)} %copy-done.19), kind=kOutput, calls=%fused_computation.12 | convolution fusion | flops 1722286080 | bytes 6883840 | tf_op jit(solution)/shard_map/dot_general | solution.py:40
  271.4 4.7 %fusion.14 = bf16[640,1024]{1,0:T(8,128)(2,1)S(1)} fusion(f32[1024,640]{0,1:T(8,128)} %copy-done.23, bf16[640,1280]{1,0:T(8,128)(2,1)S(1)} %copy-done, bf16[2,1024,1280]{2,1,0:T(8,128)(2,1)} %all-gather.2.cloned.1.call-done, f32[640]{0:T(1024)S(1)} %copy-done.19), kind=kOutput, calls=%fused_computation.29 | convolution fusion | flops 1684930560 | bytes 8194560 | tf_op jit(solution)/shard_map/dot_general | solution.py:45
  276.1 3.9 %convolution_bitcast_fusion.1 = f32[1,2,2,160,1280]{4,3,2,1,0:T(8,128)S(1)} fusion(bf16[2,2,160,1024]{3,2,1,0:T(8,128)(2,1)S(1)} %bitcast.246, bf16[2,1024,1280]{2,1,0:T(8,128)(2,1)} %all-gather.2.cloned.1.call-done), kind=kOutput, calls=%fused_computation.14 | convolution fusion | flops 1677721600 | bytes 7208960 | tf_op jit(solution)/shard_map/dot_general | solution.py:52
  280.0 4.8 %convolution_bitcast_fusion = f32[1,2,2,160,1280]{4,3,2,1,0:T(8,128)S(1)} fusion(bf16[2,2,160,1024]{3,2,1,0:T(8,128)(2,1)S(1)} %bitcast.245, bf16[2,1024,1280]{2,1,0:T(8,128)(2,1)} %all-gather.2.cloned.1.call-done), kind=kOutput, calls=%fused_computation.13 | convolution fusion | flops 1677721600 | bytes 7208960 | tf_op jit(solution)/shard_map/dot_general | solution.py:48
  284.8 1.8 fusion.67
  286.6 0.4 copy-done.6
  287.0 0.2 fusion.144
  287.3 1.9 fusion.51
  289.2 0.5 copy.103
  289.7 1.3 copy-done.1
  291.0 0.6 fusion.49
  291.6 0.1 copy.77
  291.8 0.1 copy.78
  291.9 2.4 fusion.50
  294.3 0.9 slice_bitcast_fusion.3
  295.2 0.5 collective-permute-start.7
  295.7 2.3 fusion.5
  298.0 1.7 copy-done.8
  299.7 1.6 collective-permute-start.9
  301.4 0.1 copy.73
  301.8 1.6 fusion.120
  303.4 16.6 %collective-permute-done.9 = bf16[2,160,1280]{2,1,0:T(8,128)(2,1)} collective-permute-done((bf16[2,160,1280]{2,1,0:T(8,128)(2,1)S(1)}, bf16[2,160,1280]{2,1,0:T(8,128)(2,1)}, u32[]{:S(2)}, u32[]{:S(2)}) %collective-permute-start.9) | collective-permute-done | bytes 819232 | tf_op jit(solution)/shard_map/ppermute | solution.py:77
  320.1 1.8 bitcast_add_fusion
  321.9 18.7 %reduce-scatter.2.cloned.1.call-done = bf16[128,1280]{1,0:T(8,128)(2,1)} async-done(((bf16[1024,1280]{1,0:T(8,128)(2,1)}), bf16[128,1280]{1,0:T(8,128)(2,1)}) %reduce-scatter.2.cloned.1.call-update) | async-done | bytes 327696 | tf_op jit(solution)/shard_map/reduce_scatter | solution.py:219
  340.7 1.3 fusion.130
  341.9 1.9 fusion.115
  343.9 0.6 multiply_reduce_fusion.1
  344.6 1.5 collective-permute-start
  346.2 1.3 slice_bitcast_fusion.1
  347.4 2.2 collective-permute-done
  349.7 1.2 fusion
  351.0 1.2 fusion.74
  352.3 1.3 copy.86
  (74 shorter events, 1.2 us)
Async XLA Ops:
  7.2 255.3 %copy-start = (bf16[640,1280]{1,0:T(8,128)(2,1)S(1)}, bf16[640,1280]{1,0:T(8,128)(2,1)}, u32[]{:S(2)}) copy-start(bf16[640,1280]{1,0:T(8,128)(2,1)} %param.20) | copy-start | bytes 4915204
  7.2 243.7 %all-gather.2.cloned.1.call-start = ((), (), s32[]{:S(2)}) async-start(), calls=%async_computation.1 | async-start | bytes 5898240 | tf_op jit(solution)/shard_map/all_gather | solution.py:214
  28.5 6.6 %copy-start.9 = (bf16[1,4,32,1280]{3,2,1,0:T(8,128)(2,1)S(1)}, bf16[1,4,32,1280]{3,2,1,0:T(8,128)(2,1)}, u32[]{:S(2)}) copy-start(bf16[1,4,32,1280]{3,2,1,0:T(8,128)(2,1)} %param.15) | copy-start | bytes 983044
  28.5 7.0 %copy-start.18 = (s32[8,2,2]{0,2,1:T(2,128)S(1)}, s32[8,2,2]{0,2,1:T(2,128)}, u32[]{:S(2)}) copy-start(s32[8,2,2]{0,2,1:T(2,128)} %param.26) | copy-start | bytes 388
  28.5 8.5 %copy-start.14 = (bf16[1,4,32,1280]{3,2,1,0:T(8,128)(2,1)S(1)}, bf16[1,4,32,1280]{3,2,1,0:T(8,128)(2,1)}, u32[]{:S(2)}) copy-start(bf16[1,4,32,1280]{3,2,1,0:T(8,128)(2,1)} %param.29) | copy-start | bytes 983044
  28.5 8.6 %copy-start.15 = (f32[1280]{0:T(1024)S(1)}, f32[1280]{0:T(1024)}, u32[]{:S(2)}) copy-start(f32[1280]{0:T(1024)} %param.17) | copy-start | bytes 15364
  28.5 8.6 %copy-start.16 = (f32[1280]{0:T(1024)S(1)}, f32[1280]{0:T(1024)}, u32[]{:S(2)}) copy-start(f32[1280]{0:T(1024)} %param.16) | copy-start | bytes 15364
  32.0 55.9 %collective-permute-start.1 = (bf16[4,256,1024]{2,1,0:T(8,128)(2,1)}, bf16[4,256,1024]{2,1,0:T(8,128)(2,1)}, u32[]{:S(2)}, u32[]{:S(2)}) collective-permute-start(bf16[4,256,1024]{2,1,0:T(8,128)(2,1)} %bitcast.232), channel_id=1, source_target_pairs={{0,4},{4,0},{8,12},{12,8},{16,20},{20,16},{24,28},{28,24},{1,5},{5... | collective-permute-start | bytes 6291464 | tf_op jit(solution)/shard_map/ppermute | solution.py:81
  38.3 302.4 %reduce-scatter.2.cloned.1.call-start = ((), (), s32[]{:S(2)}) async-start(), calls=%async_computation.2 | async-start | bytes 2949120 | tf_op jit(solution)/shard_map/reduce_scatter | solution.py:219
  38.4 3.6 copy-start.3
  40.3 3.9 %copy-start.10 = (bf16[1024,1024]{1,0:T(8,128)(2,1)}, bf16[1024,1024]{1,0:T(8,128)(2,1)S(1)}, u32[]{:S(2)}) copy-start(bf16[1024,1024]{1,0:T(8,128)(2,1)S(1)} %constant_dynamic-slice_fusion) | copy-start | bytes 6291460
  40.3 80.2 %collective-permute-start.3 = (bf16[1024,1024]{1,0:T(8,128)(2,1)S(1)}, bf16[1024,1024]{1,0:T(8,128)(2,1)}, u32[]{:S(2)}, u32[]{:S(2)}) collective-permute-start(bf16[1024,1024]{1,0:T(8,128)(2,1)S(1)} %constant_dynamic-slice_fusion), channel_id=1, source_target_pairs={{0,8},{4,12},{8,16},{12,20},{16,24},{20,28},{24,0},{28,4},{1,9},{5... | collective-permute-start | bytes 6291464 | tf_op jit(solution)/shard_map/ppermute | solution.py:109
  44.2 47.9 %copy-start.2 = (bf16[256,4,1,1024]{3,0,2,1:T(8,128)(2,1)}, bf16[256,4,1,1024]{3,0,2,1:T(8,128)(2,1)S(1)}, u32[]{:S(2)}) copy-start(bf16[256,4,1,1024]{3,0,2,1:T(8,128)(2,1)S(1)} %copy.130) | copy-start | bytes 6291460
  92.1 105.7 %collective-permute-start.2 = (bf16[4,512,1024]{2,1,0:T(8,128)(2,1)}, bf16[4,512,1024]{2,1,0:T(8,128)(2,1)}, u32[]{:S(2)}, u32[]{:S(2)}) collective-permute-start(bf16[4,512,1024]{2,1,0:T(8,128)(2,1)} %pad_maximum_fusion.1), channel_id=1, source_target_pairs={{0,1},{1,0},{2,3},{3,2},{4,5},{5,4},{6,7},{7,6},{8,9},{9,8},{10,11... | collective-permute-start | bytes 12582920 | tf_op jit(solution)/shard_map/ppermute | solution.py:77
  120.5 77.3 %collective-permute-start.4 = (bf16[1024,1024]{1,0:T(8,128)(2,1)}, bf16[1024,1024]{1,0:T(8,128)(2,1)}, u32[]{:S(2)}, u32[]{:S(2)}) collective-permute-start(bf16[1024,1024]{1,0:T(8,128)(2,1)} %collective-permute-done.3), channel_id=1, source_target_pairs={{0,8},{4,12},{8,16},{12,20},{16,24},{20,28},{24,0},{28,4},{1,9},{5... | collective-permute-start | bytes 6291464 | tf_op jit(solution)/shard_map/ppermute | solution.py:109
  131.7 70.2 %copy-start.11 = (bf16[1024,1024]{1,0:T(8,128)(2,1)S(1)}, bf16[1024,1024]{1,0:T(8,128)(2,1)}, u32[]{:S(2)}) copy-start(bf16[1024,1024]{1,0:T(8,128)(2,1)} %copy-done.10) | copy-start | bytes 6291460
  197.8 46.6 %collective-permute-start.5 = (bf16[1024,1024]{1,0:T(8,128)(2,1)}, bf16[1024,1024]{1,0:T(8,128)(2,1)S(1)}, u32[]{:S(2)}, u32[]{:S(2)}) collective-permute-start(bf16[1024,1024]{1,0:T(8,128)(2,1)} %collective-permute-done.4), channel_id=1, source_target_pairs={{0,8},{4,12},{8,16},{12,20},{16,24},{20,28},{24,0},{28,4},{1,9},{5... | collective-permute-start | bytes 6291464 | tf_op jit(solution)/shard_map/ppermute | solution.py:109
  212.2 38.7 %copy-start.19 = (f32[640]{0:T(1024)S(1)}, f32[640]{0:T(1024)}, u32[]{:S(2)}) copy-start(f32[640]{0:T(1024)} %param.19) | copy-start | bytes 7684
  246.8 2.0 copy-start.7
  250.0 37.2 %collective-permute-start.6 = (bf16[2,256,1024]{2,1,0:T(8,128)(2,1)}, bf16[2,256,1024]{2,1,0:T(8,128)(2,1)S(1)}, u32[]{:S(2)}, u32[]{:S(2)}) collective-permute-start(bf16[2,256,1024]{2,1,0:T(8,128)(2,1)} %fusion.121), channel_id=1, source_target_pairs={{0,4},{4,0},{8,12},{12,8},{16,20},{20,16},{24,28},{28,24},{1,5},{5... | collective-permute-start | bytes 3145736 | tf_op jit(solution)/shard_map/ppermute | solution.py:81
  261.0 1.5 copy-start.23
  276.1 3.9 %copy-start.22 = (bf16[640,1024]{1,0:T(8,128)(2,1)S(1)}, bf16[640,1024]{1,0:T(8,128)(2,1)}, u32[]{:S(2)}) copy-start(bf16[640,1024]{1,0:T(8,128)(2,1)} %get-tuple-element.29) | copy-start | bytes 3932164
  280.0 4.8 %copy-start.4 = (f32[1,2,2,160,1280]{4,3,2,1,0:T(8,128)}, f32[1,2,2,160,1280]{4,3,2,1,0:T(8,128)S(1)}, u32[]{:S(2)}) copy-start(f32[1,2,2,160,1280]{4,3,2,1,0:T(8,128)S(1)} %convolution_bitcast_fusion.1) | copy-start | bytes 9830404
  284.8 2.2 copy-start.6
  284.8 2.4 copy-start.20
  287.0 8.6 %collective-permute-start.8 = (bf16[2,2,160,1280]{3,2,1,0:T(8,128)(2,1)}, bf16[2,2,160,1280]{3,2,1,0:T(8,128)(2,1)}, u32[]{:S(2)}, u32[]{:S(2)}) collective-permute-start(bf16[2,2,160,1280]{3,2,1,0:T(8,128)(2,1)} %fusion.67), channel_id=1, source_target_pairs={{0,1},{1,0},{2,3},{3,2},{4,5},{5,4},{6,7},{7,6},{8,9},{9,8},{10,11... | collective-permute-start | bytes 4915208 | tf_op jit(solution)/shard_map/ppermute | solution.py:77
  289.7 1.4 copy-start.1
  291.9 3.8 %copy-start.5 = (f32[1,2,2,160,1280]{4,3,2,1,0:T(8,128)S(1)}, f32[1,2,2,160,1280]{4,3,2,1,0:T(8,128)}, u32[]{:S(2)}) copy-start(f32[1,2,2,160,1280]{4,3,2,1,0:T(8,128)} %copy-done.4) | copy-start | bytes 9830404
  295.2 6.5 %copy-start.21 = (s32[2]{0:T(128)S(1)}, s32[2]{0:T(128)}, u32[]{:S(2)}) copy-start(s32[2]{0:T(128)} %param.28) | copy-start | bytes 28
  295.2 6.7 %collective-permute-start.7 = (bf16[256,8,128]{2,1,0:T(8,128)(2,1)}, bf16[256,8,128]{2,1,0:T(8,128)(2,1)S(1)}, u32[]{:S(2)}, u32[]{:S(2)}) collective-permute-start(bf16[256,8,128]{2,1,0:T(8,128)(2,1)} %get-tuple-element.19), channel_id=1, source_target_pairs={{0,1},{1,0},{2,3},{3,2},{4,5},{5,4},{6,7},{7,6},{8,9},{9,8},{10,11... | collective-permute-start | bytes 1572872 | tf_op jit(solution)/shard_map/ppermute | solution.py:77
  298.0 1.7 copy-start.8
  299.7 20.4 %collective-permute-start.9 = (bf16[2,160,1280]{2,1,0:T(8,128)(2,1)S(1)}, bf16[2,160,1280]{2,1,0:T(8,128)(2,1)}, u32[]{:S(2)}, u32[]{:S(2)}) collective-permute-start(bf16[2,160,1280]{2,1,0:T(8,128)(2,1)S(1)} %fusion.124), channel_id=1, source_target_pairs={{0,2},{2,0},{1,3},{3,1},{4,6},{6,4},{5,7},{7,5},{8,10},{10,8},{9,1... | collective-permute-start | bytes 2457608 | tf_op jit(solution)/shard_map/ppermute | solution.py:77
  301.8 38.8 %copy-start.17 = (f32[1280]{0:T(1024)S(1)}, f32[1280]{0:T(1024)}, u32[]{:S(2)}) copy-start(f32[1280]{0:T(1024)} %param.21) | copy-start | bytes 15364
  340.7 3.2 copy-start.12
  344.5 5.2 %copy-start.13 = (bf16[256,2,8,128]{3,2,1,0:T(8,128)(2,1)S(1)}, bf16[256,2,8,128]{3,2,1,0:T(8,128)(2,1)}, u32[]{:S(2)}) copy-start(bf16[256,2,8,128]{3,2,1,0:T(8,128)(2,1)} %fusion.120) | copy-start | bytes 3145732
  344.6 5.0 %collective-permute-start = (bf16[2,2,128,128]{2,3,1,0:T(8,128)(2,1)S(1)}, bf16[2,2,128,128]{2,3,1,0:T(8,128)(2,1)S(1)}, u32[]{:S(2)}, u32[]{:S(2)}) collective-permute-start(bf16[2,2,128,128]{2,3,1,0:T(8,128)(2,1)S(1)} %fusion.135), channel_id=1, source_target_pairs={{0,2},{2,0},{1,3},{3,1},{4,6},{6,4},{5,7},{7,5},{8,10},{10,8},{9,1... | collective-permute-start | bytes 393224 | tf_op jit(solution)/shard_map/ppermute | solution.py:77
Sparse Core Ops, SparseCore 0:
  38.4 135.6 all-gather.1
  271.5 69.1 reduce-scatter.1

commit v2 on v1

--- a/solution.py
+++ b/solution.py
@@ -2,6 +2,7 @@
 import jax.numpy as jnp
 from jax import lax
 from jax.sharding import PartitionSpec as P
+
 
 HEADS = 32
 KV_HEADS = 4
@@ -72,6 +73,7 @@
     ).astype(jnp.bfloat16)
     return (keys, values)
 
+
 def shifted(values, axis, step):
     size = lax.axis_size(axis)
     return lax.ppermute(values, axis, [(i, (i + step) % size) for i in range(size)])
@@ -83,25 +85,29 @@
 
 def share_text(text_rows):
     enc_count = lax.axis_size("enc")
-    rows, depth = text_rows.shape
+    _, depth = text_rows.shape
     side = lax.axis_index("enc") % 2
     block = depth // enc_count
-    parts = text_rows.reshape(rows, enc_count // 2, 2, block)
-    own = lax.dynamic_index_in_dim(parts, side, 2, keepdims=False).transpose(1, 0, 2)
-    away = lax.dynamic_index_in_dim(parts, 1 - side, 2, keepdims=False).transpose(1, 0, 2)
-    pair = jnp.concatenate([swapped(away), own], axis=1)
+    even = jnp.stack([text_rows[:, i * block : (i + 1) * block] for i in range(0, enc_count, 2)])
+    odd = jnp.stack([text_rows[:, i * block : (i + 1) * block] for i in range(1, enc_count, 2)])
+    own = jnp.where(side == 0, even, odd)
+    away = jnp.where(side == 0, odd, even)
+    arrived = swapped(away)
+    pair = jnp.concatenate([arrived, own], axis=1)
     return jnp.concatenate(
         [pair] + [shifted(pair, "grp", step) for step in range(1, lax.axis_size("grp"))], axis=1
     )
 
 
-def project_queries(text_blocks, weight):
+def project_queries(text_blocks, weight, before):
     grp_count = lax.axis_size("grp")
     ring = lax.axis_size("enc") // 2
     enc_count = lax.axis_size("enc")
     place = lax.axis_index("enc") // 2
     total = None
     for step in range(ring):
+        if step == max(0, ring - 2):
+            weight, _ = lax.optimization_barrier((weight, before))
         left = lax.dynamic_index_in_dim(text_blocks, (place - step) % ring, 0, keepdims=False)
         term = jnp.dot(left, weight, preferred_element_type=jnp.float32)
         total = term if total is None else total + term
@@ -126,7 +132,7 @@
 
 def share_keys(states, key_weight, value_weight, first_head, kv_local):
     dec_count = lax.axis_size("dec")
-    rows, width = states.shape
+    rows, _ = states.shape
     if dec_count == 2 and kv_local * dec_count == KV_HEADS:
         keys, values = project_heads(states, key_weight, value_weight, KV_HEADS)
         paired = jnp.stack([keys, values])
@@ -211,13 +217,18 @@
     cotangent = jnp.where(
         own_live, state_grads.reshape(img_rows, width), jnp.zeros((), state_grads.dtype)
     )
-    both = lax.all_gather(jnp.stack([normed, cotangent]), "enc", axis=1, tiled=True)
+    sent = jnp.stack([normed, cotangent])
+    text_rows, own_half, _ = lax.optimization_barrier((text_rows, own_half, sent))
+    both = lax.all_gather(sent, "enc", axis=1, tiled=True)
     gathered, all_cotangent = both[0], both[1]
     text_blocks = share_text(text_rows)
-    queries_of = project_queries(text_blocks, own_half)
     pre, hidden, partial_full = encoder_rows(gathered, fc1_weight, fc1_bias, fc2_weight)
+    partial_full = partial_full.astype(jnp.bfloat16)
+    all_cotangent, _ = lax.optimization_barrier((all_cotangent, partial_full))
+    first_term, second_term = weight_terms(gathered, pre, hidden, all_cotangent, fc2_weight)
+    queries_of = project_queries(text_blocks, own_half, second_term)
     summed = lax.psum_scatter(
-        partial_full.astype(jnp.bfloat16), "enc", scatter_dimension=0, tiled=True
+        partial_full, "enc", scatter_dimension=0, tiled=True
     ).astype(jnp.float32)
     states = (own_rows.astype(jnp.float32) + summed + fc2_bias).astype(jnp.bfloat16)
     local_heads = query_weight.shape[1] // HD
@@ -247,7 +258,6 @@
         .reshape(samples, length, local_heads * HD)
         .astype(jnp.bfloat16)
     )
-    first_term, second_term = weight_terms(gathered, pre, hidden, all_cotangent, fc2_weight)
     fc1_grad, fc2_grad = share_grads(jnp.stack([first_term, second_term]))
     return (context, fc1_grad, fc2_grad)
 

time: 361 us -> 343 us (0.950)
  local copies, waits for them, and re-layouts: 42.7 us -> 14.5 us
  waiting for transfers between devices: 208 us -> 216 us
  matrix products: 50 us -> 45.6 us
  starting transfers between devices: 20.5 us -> 24.2 us
    all_gather x1, waiting for transfers between devices: 0.01 us -> 56.9 us  [on_device(): both = lax.all_gather(sent, 'enc', axis=1, tiled=True)]
    ppermute x3, waiting for transfers between devices: 127 us -> 78.7 us  [project_queries(): lax.ppermute(weight, 'enc', [(i, (i + 2) % enc_count) for i in range(enc_...]
    ppermute x2, waiting for transfers between devices: 43.8 us -> 76.5 us  [swapped(): lax.ppermute(values, 'enc', [(i, i ^ 1) for i in range(lax.axis_size('enc...]
    dynamic_slice x3 -> x0, local copies, waits for them, and re-layouts: 19.1 us -> none  [the longest x2 16.8 us: share_text(): lax.dynamic_index_in_dim(parts, 1 - side, 2, keepdims=False)]
    reduce_scatter x1, waiting for transfers between devices: 18.7 us -> 0.02 us  [on_device(): lax.psum_scatter(partial_full, 'enc', scatter_dimension=0, tiled=True)]
    ppermute x5, waiting for transfers between devices: 18.9 us -> 3.69 us  [shifted(): lax.ppermute(values, axis, [(i, (i + step) % size) for i in range(size)])]
    dot_general x4, matrix products: 12.6 us -> 20.5 us  [project_queries(): term = jnp.dot(left, weight, preferred_element_type=jnp.float32)]
    another operation x1, local copies, waits for them, and re-layouts: 7.91 us -> 0.64 us  [share_text(): jnp.stack([text_rows[:, i * block:(i + 1) * block] for i in range(1, enc_...]
  transfers between devices with their start and end apart: 12 -> 12, of which waited for: 7 -> 6; matrix products, arithmetic and copies ran while one was open for 22% -> 21% of each run, Pallas kernels for 0% -> 0%
where the time goes in v2:
time: 343 us; the launch traced here: 342 us
  waiting for transfers between devices  216 us (63%)
  matrix products  45.6 us (13%)
  other arithmetic  27.6 us (8%)
  starting transfers between devices  24.2 us (7%)
  local copies, waits for them, and re-layouts  14.5 us (4%)
  between operations  14.5 us (4%)
    ppermute x3, waiting for transfers between devices, project_queries(): lax.ppermute(weight, 'enc', [(i, (i + 2) % enc_count) for i in range(enc_...  78.7 us
    ppermute x2, waiting for transfers between devices, swapped(): lax.ppermute(values, 'enc', [(i, i ^ 1) for i in range(lax.axis_size('enc...  76.5 us
    all_gather x1, waiting for transfers between devices, on_device(): both = lax.all_gather(sent, 'enc', axis=1, tiled=True)  56.9 us
    dot_general x4, matrix products, project_queries(): term = jnp.dot(left, weight, preferred_element_type=jnp.float32)  20.5 us
    ppermute x3, starting transfers between devices, project_queries(): lax.ppermute(weight, 'enc', [(i, (i + 2) % enc_count) for i in range(enc_...  17.4 us
    dot_general x1, matrix products, encoder_rows(): lax.dot_general(rows, fc1_weight, (((1,), (1,)), ((), ())), preferred_ele...  9.74 us
  transfers between devices with their start and end apart: 12, of which 6 were waited for; matrix products, arithmetic and copies ran while one was open for 21% of the time, Pallas kernels for 0%

profile of v2, /device:TPU:0, one launch (start us, length us, event | category | flops | bytes accessed | tf_op | source)
XLA Modules:
  0.0 342.3 jit_solution(1670016087276113282)
XLA Ops:
  7.2 1.2 convert_reduce_fusion
  8.5 0.1 div.44
  8.5 1.2 multiply_reduce_fusion
  9.7 1.3 dynamic_slice.45
  11.0 0.6 iota_compare_fusion.2
  11.7 0.1 broadcast_in_dim.40
  11.8 0.1 rsqrt.28
  11.9 1.1 bitcast_select_fusion.2
  13.0 1.3 fusion.75
  14.3 0.9 pad_maximum_fusion.4
  15.3 3.3 constant_dynamic-slice_fusion
  18.5 0.6 slice_bitcast_fusion.13
  19.2 2.3 broadcast_select_fusion.1
  21.5 3.0 collective-permute-start.1
  24.5 1.6 collective-permute-start.3
  26.0 0.1 copy.56
  26.2 0.2 fusion.91
  26.4 0.1 broadcast_in_dim.70
  26.5 0.1 and.58
  26.6 0.1 iota_compare_fusion.1
  26.7 50.7 %collective-permute-done.1 = bf16[4,256,1024]{2,1,0:T(8,128)(2,1)} collective-permute-done((bf16[4,256,1024]{2,1,0:T(8,128)(2,1)}, bf16[4,256,1024]{2,1,0:T(8,128)(2,1)}, u32[]{:S(2)}, u32[]{:S(2)}) %collective-permute-start.1) | collective-permute-done | bytes 2097184 | tf_op jit(solution)/shard_map/ppermute | solution.py:83
  77.4 5.0 %pad_maximum_fusion.1 = bf16[4,512,1024]{2,1,0:T(8,128)(2,1)} fusion(bf16[4,256,1024]{2,1,0:T(8,128)(2,1)} %get-tuple-element.21, bf16[4,256,1024]{2,1,0:T(8,128)(2,1)} %collective-permute-done.1), kind=kLoop, calls=%fused_computation.5 | loop fusion | flops 8388608 | bytes 8388608 | tf_op jit(solution)/shard_map/concatenate | solution.py:96
  82.4 27.4 %collective-permute-done.3 = bf16[1024,1024]{1,0:T(8,128)(2,1)} collective-permute-done((bf16[1024,1024]{1,0:T(8,128)(2,1)}, bf16[1024,1024]{1,0:T(8,128)(2,1)}, u32[]{:S(2)}, u32[]{:S(2)}) %collective-permute-start.3) | collective-permute-done | bytes 2097184 | tf_op jit(solution)/shard_map/ppermute | solution.py:115
  109.8 15.8 %collective-permute-start.4 = (bf16[1024,1024]{1,0:T(8,128)(2,1)}, bf16[1024,1024]{1,0:T(8,128)(2,1)}, u32[]{:S(2)}, u32[]{:S(2)}) collective-permute-start(bf16[1024,1024]{1,0:T(8,128)(2,1)} %collective-permute-done.3), channel_id=1, source_target_pairs={{0,8},{4,12},{8,16},{12,20},{16,24},{20,28},{24,0},{28,4},{1,9},{5... | collective-permute-start | bytes 6291464 | tf_op jit(solution)/shard_map/ppermute | solution.py:115
  125.6 56.9 %all-gather.2.cloned.1.call-done = bf16[2,1024,1280]{2,1,0:T(8,128)(2,1)} async-done(((bf16[2,128,1280]{2,1,0:T(8,128)(2,1)}), bf16[2,1024,1280]{2,1,0:T(8,128)(2,1)}) %all-gather.2.cloned.1.call-update) | async-done | bytes 5242896 | tf_op jit(solution)/shard_map/all_gather | solution.py:222
  182.5 9.7 %fusion.8 = (bf16[1024,640]{0,1:T(8,128)(2,1)S(1)}, f32[1024,640]{0,1:T(8,128)}) fusion(f32[640]{0:T(1024)S(1)} %copy-done.13, bf16[640,1280]{1,0:T(8,128)(2,1)S(1)} %copy-done.11, bf16[2,1024,1280]{2,1,0:T(8,128)(2,1)} %all-gather.2.cloned.1.call-done), kind=kOutput, calls=%fused_computation.21 | convolution fusion | flops 1720975360 | bytes 8194560 | tf_op jit(solution)/shard_map/dot_general | solution.py:35
  192.3 1.1 copy-done.16
  193.3 3.8 %convolution_convert_fusion = bf16[1024,1280]{1,0:T(8,128)(2,1)} fusion(bf16[1024,640]{0,1:T(8,128)(2,1)S(1)} %get-tuple-element.38, bf16[640,1280]{1,0:T(8,128)(2,1)S(1)} %copy-done), kind=kOutput, calls=%fused_computation.11 | convolution fusion | flops 1679032320 | bytes 5570560 | tf_op jit(solution)/shard_map/dot_general | solution.py:41
  197.1 2.1 slice_bitcast_fusion
  199.2 4.0 %fusion.14 = bf16[640,1024]{1,0:T(8,128)(2,1)S(1)} fusion(f32[1024,640]{0,1:T(8,128)} %get-tuple-element.39, bf16[1024,1280]{1,0:T(8,128)(2,1)S(1)} %slice_bitcast_fusion, bf16[640,1280]{1,0:T(8,128)(2,1)S(1)} %copy-done, f32[640]{0:T(1024)S(1)} %copy-done.13), kind=kOutput, calls=%fused_computation.27 | convolution fusion | flops 1684930560 | bytes 8194560 | tf_op jit(solution)/shard_map/dot_general | solution.py:46
  203.3 1.9 fusion.92
  205.2 1.9 convolution_bitcast_fusion
  207.1 1.5 fusion.48
  208.6 0.9 copy-done.3
  209.5 0.7 copy-done.2
  210.2 6.5 %pad_maximum_fusion = bf16[4,1024,1024]{2,1,0:T(8,128)(2,1)} fusion(bf16[4,512,1024]{2,1,0:T(8,128)(2,1)} %collective-permute-done.2, bf16[4,256,1024]{2,1,0:T(8,128)(2,1)S(1)} %copy-done.2, bf16[4,256,1024]{2,1,0:T(8,128)(2,1)} %collective-permute-done.1), kind=kLoop, calls=%fused_computation | loop fusion | flops 25165824 | bytes 16777216 | tf_op jit(solution)/shard_map/concatenate | solution.py:97
  216.7 6.6 %fusion.40 = f32[1024,1024]{1,0:T(8,128)} fusion(bf16[1024,1024]{1,0:T(8,128)(2,1)} %constant_dynamic-slice_fusion, bf16[4,1024,1024]{2,1,0:T(8,128)(2,1)} %pad_maximum_fusion, s32[]{:T(128)S(6)} %select_n.141), kind=kOutput, calls=%fused_computation.74 | convolution fusion | flops 2147483648 | bytes 8388612 | tf_op jit(solution)/shard_map/dot_general | solution.py:112
  223.3 4.6 %fusion.38 = f32[1024,1024]{1,0:T(8,128)S(1)} fusion(bf16[1024,1024]{1,0:T(8,128)(2,1)} %collective-permute-done.3, bf16[4,1024,1024]{2,1,0:T(8,128)(2,1)} %pad_maximum_fusion, s32[]{:T(128)S(6)} %select_n.143), kind=kOutput, calls=%fused_computation.72 | convolution fusion | flops 2147483648 | bytes 8388612 | tf_op jit(solution)/shard_map/dot_general | solution.py:112
  227.9 4.7 %fusion.36 = f32[1024,1024]{1,0:T(8,128)S(1)} fusion(bf16[1024,1024]{1,0:T(8,128)(2,1)} %collective-permute-done.4, bf16[4,1024,1024]{2,1,0:T(8,128)(2,1)} %pad_maximum_fusion, s32[]{:T(128)S(6)} %select_n.145), kind=kOutput, calls=%fused_computation.70 | convolution fusion | flops 2147483648 | bytes 8388612 | tf_op jit(solution)/shard_map/dot_general | solution.py:112
  232.6 1.9 fusion.5
  234.5 0.1 fusion.71
  234.6 1.6 collective-permute-start.9
  236.2 51.3 %collective-permute-done.5 = bf16[1024,1024]{1,0:T(8,128)(2,1)} collective-permute-done((bf16[1024,1024]{1,0:T(8,128)(2,1)}, bf16[1024,1024]{1,0:T(8,128)(2,1)}, u32[]{:S(2)}, u32[]{:S(2)}) %collective-permute-start.5) | collective-permute-done | bytes 2097184 | tf_op jit(solution)/shard_map/ppermute | solution.py:115
  287.5 4.7 %add_add_fusion = f32[1024,1024]{1,0:T(8,128)S(1)} fusion(f32[1024,1024]{1,0:T(8,128)S(1)} %fusion.36, f32[1024,1024]{1,0:T(8,128)S(1)} %copy-done.7, f32[1024,1024]{1,0:T(8,128)S(1)} %fusion.38, bf16[1024,1024]{1,0:T(8,128)(2,1)} %collective-permute-done.5, bf16[4,1024,1024]{2,1,0:T(8,128)(2,1)} %pad_maximum_fusion, s32[]{:T(128)S(6)} %select_n.147), kind=kOutput, calls=%fused_computation.8 | convolution fusion | flops 2150629376 | bytes 20971524 | tf_op jit(solution)/shard_map/dot_general | solution.py:112
  292.2 0.2 fusion.68
  292.4 0.6 collective-permute-start.6
  293.0 0.1 bitcast_add_fusion
  293.1 1.3 slice_bitcast_fusion.2
  294.4 25.8 %collective-permute-done.6 = bf16[2,256,1024]{2,1,0:T(8,128)(2,1)S(1)} collective-permute-done((bf16[2,256,1024]{2,1,0:T(8,128)(2,1)S(1)}, bf16[2,256,1024]{2,1,0:T(8,128)(2,1)S(1)}, u32[]{:S(2)}, u32[]{:S(2)}) %collective-permute-start.6) | collective-permute-done | bytes 1048608 | tf_op jit(solution)/shard_map/ppermute | solution.py:83
  320.2 0.3 fusion.32
  320.5 0.5 copy.83
  321.0 0.6 fusion.30
  321.6 0.1 copy.58
  321.7 0.1 copy.59
  321.9 1.0 fusion.31
  323.1 1.2 fusion.77
  324.3 0.6 multiply_reduce_fusion.1
  324.9 0.6 fusion.62
  325.6 1.6 collective-permute-start
  327.2 0.6 fusion.67
  327.8 3.7 %collective-permute-done = bf16[2,2,128,128]{2,3,1,0:T(8,128)(2,1)S(1)} collective-permute-done((bf16[2,2,128,128]{2,3,1,0:T(8,128)(2,1)S(1)}, bf16[2,2,128,128]{2,3,1,0:T(8,128)(2,1)S(1)}, u32[]{:S(2)}, u32[]{:S(2)}) %collective-permute-start) | collective-permute-done | bytes 131104 | tf_op jit(solution)/shard_map/ppermute | solution.py:79
  331.6 1.2 fusion
  332.8 1.2 fusion.53
  334.1 1.3 copy.67
  (66 shorter events, 0.8 us)
Async XLA Ops:
  7.2 186.2 %copy-start = (bf16[640,1280]{1,0:T(8,128)(2,1)S(1)}, bf16[640,1280]{1,0:T(8,128)(2,1)}, u32[]{:S(2)}) copy-start(bf16[640,1280]{1,0:T(8,128)(2,1)} %param.20) | copy-start | bytes 4915204
  7.2 175.3 %all-gather.2.cloned.1.call-start = ((), (), s32[]{:S(2)}) async-start(), calls=%async_computation.1 | async-start | bytes 5898240 | tf_op jit(solution)/shard_map/all_gather | solution.py:222
  15.2 307.8 %reduce-scatter.2.cloned.1.call-start = ((), (), s32[]{:S(2)}) async-start(), calls=%async_computation.2 | async-start | bytes 2949120 | tf_op jit(solution)/shard_map/reduce_scatter | solution.py:230
  15.3 3.3 copy-start.6
  19.2 6.9 %copy-start.14 = (s32[2,2]{1,0:T(2,128)S(1)}, s32[2,2]{1,0:T(2,128)}, u32[]{:S(2)}) copy-start(s32[2,2]{1,0:T(2,128)} %param.27) | copy-start | bytes 52
  19.2 7.0 %copy-start.10 = (s32[8,2,2]{0,2,1:T(2,128)S(1)}, s32[8,2,2]{0,2,1:T(2,128)}, u32[]{:S(2)}) copy-start(s32[8,2,2]{0,2,1:T(2,128)} %param.26) | copy-start | bytes 388
  19.2 7.4 %copy-start.15 = (s32[2]{0:T(128)S(1)}, s32[2]{0:T(128)}, u32[]{:S(2)}) copy-start(s32[2]{0:T(128)} %param.28) | copy-start | bytes 28
  21.5 55.9 %collective-permute-start.1 = (bf16[4,256,1024]{2,1,0:T(8,128)(2,1)}, bf16[4,256,1024]{2,1,0:T(8,128)(2,1)}, u32[]{:S(2)}, u32[]{:S(2)}) collective-permute-start(bf16[4,256,1024]{2,1,0:T(8,128)(2,1)} %get-tuple-element.20), channel_id=1, source_target_pairs={{0,4},{4,0},{8,12},{12,8},{16,20},{20,16},{24,28},{28,24},{1,5},{5... | collective-permute-start | bytes 6291464 | tf_op jit(solution)/shard_map/ppermute | solution.py:83
  24.5 85.3 %collective-permute-start.3 = (bf16[1024,1024]{1,0:T(8,128)(2,1)}, bf16[1024,1024]{1,0:T(8,128)(2,1)}, u32[]{:S(2)}, u32[]{:S(2)}) collective-permute-start(bf16[1024,1024]{1,0:T(8,128)(2,1)} %constant_dynamic-slice_fusion), channel_id=1, source_target_pairs={{0,8},{4,12},{8,16},{12,20},{16,24},{20,28},{24,0},{28,4},{1,9},{5... | collective-permute-start | bytes 6291464 | tf_op jit(solution)/shard_map/ppermute | solution.py:115
  77.4 105.1 %copy-start.11 = (bf16[640,1280]{1,0:T(8,128)(2,1)S(1)}, bf16[640,1280]{1,0:T(8,128)(2,1)}, u32[]{:S(2)}) copy-start(bf16[640,1280]{1,0:T(8,128)(2,1)} %param.18) | copy-start | bytes 4915204
  77.4 105.1 %copy-start.13 = (f32[640]{0:T(1024)S(1)}, f32[640]{0:T(1024)}, u32[]{:S(2)}) copy-start(f32[640]{0:T(1024)} %param.19) | copy-start | bytes 7684
  82.4 127.1 %collective-permute-start.2 = (bf16[4,512,1024]{2,1,0:T(8,128)(2,1)}, bf16[4,512,1024]{2,1,0:T(8,128)(2,1)}, u32[]{:S(2)}, u32[]{:S(2)}) collective-permute-start(bf16[4,512,1024]{2,1,0:T(8,128)(2,1)} %pad_maximum_fusion.1), channel_id=1, source_target_pairs={{0,1},{1,0},{2,3},{3,2},{4,5},{5,4},{6,7},{7,6},{8,9},{9,8},{10,11... | collective-permute-start | bytes 12582920 | tf_op jit(solution)/shard_map/ppermute | solution.py:79
  109.8 106.9 %collective-permute-start.4 = (bf16[1024,1024]{1,0:T(8,128)(2,1)}, bf16[1024,1024]{1,0:T(8,128)(2,1)}, u32[]{:S(2)}, u32[]{:S(2)}) collective-permute-start(bf16[1024,1024]{1,0:T(8,128)(2,1)} %collective-permute-done.3), channel_id=1, source_target_pairs={{0,8},{4,12},{8,16},{12,20},{16,24},{20,28},{24,0},{28,4},{1,9},{5... | collective-permute-start | bytes 6291464 | tf_op jit(solution)/shard_map/ppermute | solution.py:115
  192.3 1.1 copy-start.16
  197.1 8.0 %slice-start = ((s8[5242880]{0:T(1024)(128)(4,1)}), s8[4194304]{0:T(1024)(128)(4,1)S(1)}, s32[]{:S(2)}) async-start(s8[5242880]{0:T(1024)(128)(4,1)} %bitcast.207), calls=%async_computation.3 | async-start | bytes 8388608
  199.2 4.1 %copy-start.17 = (bf16[1024,640]{0,1:T(8,128)(2,1)S(1)}, bf16[1024,640]{0,1:T(8,128)(2,1)}, u32[]{:S(2)}) copy-start(bf16[1024,640]{0,1:T(8,128)(2,1)} %copy-done.16) | copy-start | bytes 3932164
  199.2 5.9 %slice-start.1 = ((s8[5242880]{0:T(1024)(128)(4,1)}), s8[1048576]{0:T(1024)(128)(4,1)S(1)}, s32[]{:S(2)}) async-start(s8[5242880]{0:T(1024)(128)(4,1)} %bitcast.207), calls=%async_computation.4 | async-start | bytes 2097152
  207.1 2.4 copy-start.3
  207.1 3.2 copy-start.2
  209.5 23.1 %collective-permute-start.8 = (bf16[2,2,160,1280]{3,2,1,0:T(8,128)(2,1)}, bf16[2,2,160,1280]{3,2,1,0:T(8,128)(2,1)}, u32[]{:S(2)}, u32[]{:S(2)}) collective-permute-start(bf16[2,2,160,1280]{3,2,1,0:T(8,128)(2,1)} %fusion.48), channel_id=1, source_target_pairs={{0,1},{1,0},{2,3},{3,2},{4,5},{5,4},{6,7},{7,6},{8,9},{9,8},{10,11... | collective-permute-start | bytes 4915208 | tf_op jit(solution)/shard_map/ppermute | solution.py:79
  216.7 70.8 %collective-permute-start.5 = (bf16[1024,1024]{1,0:T(8,128)(2,1)}, bf16[1024,1024]{1,0:T(8,128)(2,1)}, u32[]{:S(2)}, u32[]{:S(2)}) collective-permute-start(bf16[1024,1024]{1,0:T(8,128)(2,1)} %collective-permute-done.4), channel_id=1, source_target_pairs={{0,8},{4,12},{8,16},{12,20},{16,24},{20,28},{24,0},{28,4},{1,9},{5... | collective-permute-start | bytes 6291464 | tf_op jit(solution)/shard_map/ppermute | solution.py:115
  227.9 4.7 %copy-start.4 = (f32[1,2,2,160,1280]{4,3,2,1,0:T(8,128)S(1)}, f32[1,2,2,160,1280]{4,3,2,1,0:T(8,128)}, u32[]{:S(2)}) copy-start(f32[1,2,2,160,1280]{4,3,2,1,0:T(8,128)} %copy-done.3) | copy-start | bytes 9830404
  232.6 54.9 %copy-start.7 = (f32[1024,1024]{1,0:T(8,128)S(1)}, f32[1024,1024]{1,0:T(8,128)}, u32[]{:S(2)}) copy-start(f32[1024,1024]{1,0:T(8,128)} %fusion.40) | copy-start | bytes 12582916
  234.6 58.3 %collective-permute-start.9 = (bf16[2,160,1280]{2,1,0:T(8,128)(2,1)S(1)}, bf16[2,160,1280]{2,1,0:T(8,128)(2,1)S(1)}, u32[]{:S(2)}, u32[]{:S(2)}) collective-permute-start(bf16[2,160,1280]{2,1,0:T(8,128)(2,1)S(1)} %fusion.71), channel_id=1, source_target_pairs={{0,2},{2,0},{1,3},{3,1},{4,6},{6,4},{5,7},{7,5},{8,10},{10,8},{9,1... | collective-permute-start | bytes 2457608 | tf_op jit(solution)/shard_map/ppermute | solution.py:79
  292.4 27.8 %collective-permute-start.6 = (bf16[2,256,1024]{2,1,0:T(8,128)(2,1)S(1)}, bf16[2,256,1024]{2,1,0:T(8,128)(2,1)S(1)}, u32[]{:S(2)}, u32[]{:S(2)}) collective-permute-start(bf16[2,256,1024]{2,1,0:T(8,128)(2,1)S(1)} %fusion.68), channel_id=1, source_target_pairs={{0,4},{4,0},{8,12},{12,8},{16,20},{20,16},{24,28},{28,24},{1,5},{5... | collective-permute-start | bytes 3145736 | tf_op jit(solution)/shard_map/ppermute | solution.py:83
  321.8 1.2 copy-start.5
  321.8 1.2 copy-start.9
  322.8 1.4 copy-start.8
  322.9 4.3 %collective-permute-start.7 = (bf16[256,8,128]{2,1,0:T(8,128)(2,1)S(1)}, bf16[256,8,128]{2,1,0:T(8,128)(2,1)S(1)}, u32[]{:S(2)}, u32[]{:S(2)}) collective-permute-start(bf16[256,8,128]{2,1,0:T(8,128)(2,1)S(1)} %get-tuple-element.32), channel_id=1, source_target_pairs={{0,1},{1,0},{2,3},{3,2},{4,5},{5,4},{6,7},{7,6},{8,9},{9,8},{10,11... | collective-permute-start | bytes 1572872 | tf_op jit(solution)/shard_map/ppermute | solution.py:79
  323.0 1.9 copy-start.12
  325.6 5.9 %collective-permute-start = (bf16[2,2,128,128]{2,3,1,0:T(8,128)(2,1)S(1)}, bf16[2,2,128,128]{2,3,1,0:T(8,128)(2,1)S(1)}, u32[]{:S(2)}, u32[]{:S(2)}) collective-permute-start(bf16[2,2,128,128]{2,3,1,0:T(8,128)(2,1)S(1)} %fusion.82), channel_id=1, source_target_pairs={{0,2},{2,0},{1,3},{3,1},{4,6},{6,4},{5,7},{7,5},{8,10},{10,8},{9,1... | collective-permute-start | bytes 393224 | tf_op jit(solution)/shard_map/ppermute | solution.py:79
  332.8 2.6 copy-start.1
Sparse Core Ops, SparseCore 0:
  15.3 167.1 all-gather.1
  223.4 93.4 reduce-scatter.1
